TPU v7x, 32 devices: a whole 2x2x4 slice. The times are simulated.
32 devices in a mesh: row: 8 (over z, x), col: 4 (over y, core).
Axes of the slice: x: 2, y: 2, z: 4, core: 2. Of those that a mesh axis runs over, the one named last changes fastest.
Arguments:
- acquired_tiles: bfloat16 [4, 32768, 1024], P(None, ('row', 'col')), may hold values from -24 to 24
- row_live: int32 [4, 32768], P(None, ('row', 'col')), may hold values from 0 to 1, as said below
- col_live: int32 [4, 32768], P(None, ('row', 'col')), may hold values 0 or 1
- row_order: int32 [8], replicated, may hold values from 0 to 7, as said below
- source_init: float32 [32768, 256], P(('row', 'col')), may hold values from -3 to 3
- receiver_init: float32 [32768, 256], P(('row', 'col')), may hold values from -3 to 3
Outputs:
- sources: float32 [32768, 256], P(('row', 'col'))
- receivers: float32 [32768, 256], P(('row', 'col'))
Inputs may be any that keep to these rules, and one draw needn't show every extreme that they name: `row_live`: 1 where the source of that row is recorded in that stratum's tile; sources go missing singly and in whole aligned lines of 128 rows, and the share of missing lines differs from block to block. `row_order`: each number once.
All inputs are finite; a program needn't handle non-finite values. No bound on the sum of `col_live` on one device may be relied on, other than what follows from the above.
Results may differ from a plain program's by a relative error of at most 0.00096.
Values sent between devices are 32-bit elements; how exact they have to be, the bound alone decides.
A program may use at most 128 MiB of HBM per device.

v0:
```python
import functools

import jax
import jax.numpy as jnp
from jax import lax
from jax.experimental import pallas as pl
from jax.experimental.pallas import tpu as pltpu
from jax.sharding import PartitionSpec as P

STEPS = 2
MESH = pl.DeviceIdType.MESH
F32 = jnp.float32
BF16 = jnp.bfloat16


def kernel(nr, nc, tiles, row_live, col_live, order, src_in, rec_in, src_out, rec_out,
           tile, rb, mid, out2, grad, half, half_t, row_mask,
           in_sem, ring_send, ring_recv, a_send, a_recv, b_send, b_recv):
    strata, block, width = tile.shape
    rank = src_out.shape[1]
    chunk = rb.shape[2]
    chunks = width // chunk
    piece = mid.shape[1]
    per_chunk = nr // chunks
    step_size = 1.0 / (width + 2 * rank)
    r = lax.axis_index("row")
    c = lax.axis_index("col")
    cn = lax.rem(c + 1, nc)
    rn = lax.rem(r + (c + 1) // nc, nr)
    cp = lax.rem(c + nc - 1, nc)

    loads = [
        pltpu.make_async_copy(tiles.at[s], tile.at[s], in_sem.at[s]) for s in range(strata)
    ]
    for load in loads:
        load.start()

    barrier = pltpu.get_barrier_semaphore()
    for k in range(nr):
        pl.semaphore_signal(barrier, inc=1, device_id={"row": k, "col": cp}, device_id_type=MESH)
    for k in range(1, nr):
        pl.semaphore_signal(
            barrier, inc=1, device_id={"row": lax.rem(r + k, nr), "col": c}, device_id_type=MESH
        )

    src_out[...] = src_in[...]
    for q in range(chunks):
        rb[0, q * rank:(q + 1) * rank, :] = rec_in[q * chunk:(q + 1) * chunk, :].T

    def ring_copy(s, q):
        lane = 0 if s == 0 else 1
        rows = pl.ds(q * rank, rank)
        return pltpu.make_async_remote_copy(
            src_ref=rb.at[s, rows], dst_ref=rb.at[s + 1, rows],
            send_sem=ring_send.at[lane, q], recv_sem=ring_recv.at[lane, q],
            device_id={"row": rn, "col": cn}, device_id_type=MESH,
        )

    def a_copy(s, p, slot):
        return pltpu.make_async_remote_copy(
            src_ref=rb.at[s, pl.ds(p * piece, piece)], dst_ref=mid.at[slot],
            send_sem=a_send.at[p], recv_sem=a_recv.at[slot],
            device_id={"row": p, "col": cn}, device_id_type=MESH,
        )

    def b_copy(s, to, p):
        return pltpu.make_async_remote_copy(
            src_ref=out2.at[to], dst_ref=rb.at[s + 1, pl.ds(p * piece, piece)],
            send_sem=b_send.at[to], recv_sem=b_recv.at[p],
            device_id={"row": to, "col": c}, device_id_type=MESH,
        )

    for s in range(strata):
        lanes = row_live[s:s + 1, :].astype(F32)
        for t in range(block // 128):
            row_mask[t * 128:(t + 1) * 128, :] = jnp.broadcast_to(
                lanes[:, t * 128:(t + 1) * 128], (128, 128)
            ).T * step_size
        loads[s].wait()
        for it in range(STEPS):
            half[...] = src_out[...].astype(BF16)
            half_t[...] = (src_out[...].T * lanes).astype(BF16)

            def one(q, carry, s=s, it=it):
                rows = pl.ds(pl.multiple_of(q * rank, rank), rank)
                cols = pl.ds(pl.multiple_of(q * chunk, chunk), chunk)
                if it == 0 and s > 0:
                    if s == 2:
                        for j in range(per_chunk):
                            p = q * per_chunk + j

                            @pl.when(p != r)
                            def _():
                                b_copy(1, r, p).wait_recv()
                    else:
                        ring_copy(s - 1, q).wait_recv()
                rec = rb[s, rows, :]
                rec_half = rec.astype(BF16)
                live = col_live[s:s + 1, cols].astype(F32)
                predicted = jnp.dot(half[...], rec_half, preferred_element_type=F32)
                misfit = (tile[s, :, cols].astype(F32) - predicted).astype(BF16)
                grad_rec = jnp.dot(half_t[...], misfit, preferred_element_type=F32)
                rb[s, rows, :] = rec + (step_size * live) * grad_rec
                grad_src = lax.dot_general(
                    misfit, (rec_half * live.astype(BF16)), (((1,), (1,)), ((), ())),
                    preferred_element_type=F32,
                )

                @pl.when(q == 0)
                def _():
                    grad[...] = grad_src

                @pl.when(q > 0)
                def _():
                    grad[...] += grad_src

                if it == STEPS - 1 and s in (0, 2):
                    ring_copy(s, q).start()
                return carry

            if s == 0 and it == 0:
                pass
            if it == STEPS - 1 and s == 0:
                pl.semaphore_wait(barrier, 2 * nr - 1)
            lax.fori_loop(0, chunks, one, 0)
            if it == STEPS - 1 and s == 1:
                def send_a(k, carry):
                    p = lax.rem(r + k, nr)
                    a_copy(1, p, rn).start()
                    return carry
                lax.fori_loop(0, nr, send_a, 0)
            for h in range(rank // 128):
                part = slice(h * 128, (h + 1) * 128)
                src_out[:, part] = src_out[:, part] + row_mask[...] * grad[:, part]
        if s == 1:
            def wait_a(k, carry):
                a_copy(1, 0, k).wait_recv()
                return carry
            lax.fori_loop(0, nr, wait_a, 0)
            rb[2, pl.ds(pl.multiple_of(r * piece, piece), piece), :] = mid[order[r]]

            def pick(k, carry):
                to = lax.rem(r + k, nr)
                out2[to] = mid[order[to]]
                return carry
            lax.fori_loop(1, nr, pick, 0)

            def send_b(k, carry):
                b_copy(1, lax.rem(r + k, nr), r).start()
                return carry
            lax.fori_loop(1, nr, send_b, 0)

    for q in range(chunks):
        rec_out[q * chunk:(q + 1) * chunk, :] = rb[strata - 1, q * rank:(q + 1) * rank, :].T
    for s in (0, 2):
        for q in range(chunks):
            ring_copy(s, q).wait_send()

    def done_a(k, carry):
        a_copy(1, k, 0).wait_send()
        return carry
    lax.fori_loop(0, nr, done_a, 0)

    def done_b(k, carry):
        b_copy(1, lax.rem(r + k, nr), r).wait_send()
        return carry
    lax.fori_loop(1, nr, done_b, 0)


def local(nr, nc, tiles, row_live, col_live, row_order, source_init, receiver_init):
    strata, block, width = tiles.shape
    rank = source_init.shape[1]
    chunk = width // 4
    chunks = width // chunk
    piece = chunks * rank // nr
    vmem = pl.BlockSpec(memory_space=pltpu.VMEM)
    return pl.pallas_call(
        functools.partial(kernel, nr, nc),
        out_shape=(
            jax.ShapeDtypeStruct(source_init.shape, F32),
            jax.ShapeDtypeStruct(receiver_init.shape, F32),
        ),
        in_specs=[
            pl.BlockSpec(memory_space=pl.ANY), vmem, vmem,
            pl.BlockSpec(memory_space=pltpu.SMEM), vmem, vmem,
        ],
        out_specs=(vmem, vmem),
        scratch_shapes=[
            pltpu.VMEM((strata, block, width), BF16),
            pltpu.VMEM((strata, chunks * rank, chunk), F32),
            pltpu.VMEM((nr, piece, chunk), F32),
            pltpu.VMEM((nr, piece, chunk), F32),
            pltpu.VMEM((block, rank), F32),
            pltpu.VMEM((block, rank), BF16),
            pltpu.VMEM((rank, block), BF16),
            pltpu.VMEM((block, 128), F32),
            pltpu.SemaphoreType.DMA((strata,)),
            pltpu.SemaphoreType.DMA((2, chunks)),
            pltpu.SemaphoreType.DMA((2, chunks)),
            pltpu.SemaphoreType.DMA((nr,)),
            pltpu.SemaphoreType.DMA((nr,)),
            pltpu.SemaphoreType.DMA((nr,)),
            pltpu.SemaphoreType.DMA((nr,)),
        ],
        compiler_params=pltpu.CompilerParams(
            collective_id=0, has_side_effects=True, vmem_limit_bytes=56 * 1024 * 1024
        ),
    )(tiles, row_live, col_live, row_order, source_init, receiver_init)


def solution(mesh):
    placed = (
        P(None, ("row", "col"), None),
        P(None, ("row", "col")),
        P(None, ("row", "col")),
        P(),
        P(("row", "col"), None),
        P(("row", "col"), None),
    )
    return jax.shard_map(
        functools.partial(local, mesh.shape["row"], mesh.shape["col"]),
        mesh=mesh,
        in_specs=placed,
        out_specs=(P(("row", "col"), None), P(("row", "col"), None)),
        check_vma=False,
    )
```

profile of v0, /device:TPU:0, one launch (start us, length us, event | category | flops | bytes accessed | tf_op | source)
XLA Modules:
  0.0 101.7 jit_solution(15714195741315128148)
XLA Ops:
  0.6 96.5 %shard_map.77 = (f32[1024,256]{1,0:T(8,128)}, f32[1024,256]{1,0:T(8,128)}) custom-call(bf16[4,1024,1024]{2,1,0:T(8,128)(2,1)} %tiles.1, s32[4,1024]{1,0:T(4,128)} %row_live.1, s32[4,1024]{1,0:T(4,128)} %col_live.1, s32[8]{0:T(128)} %order.1, f32[1024,256]{1,0:T(8,128)} %src_in.1, f32[1024,256]{1,0:T(8,128)} %rec_in.1), custom_call_target="tpu_custom_call" | custom-call | tf_op jit(solution)/shard_map/pallas_call | solution.py:177
  97.2 2.3 %copy.10 = f32[1024,256]{1,0:T(8,128)} copy(f32[1024,256]{1,0:T(8,128)} %get-tuple-element.4) | data formatting | bytes 2097152
  99.4 2.3 %copy.11 = f32[1024,256]{1,0:T(8,128)} copy(f32[1024,256]{1,0:T(8,128)} %get-tuple-element.5) | data formatting | bytes 2097152
where the time goes:
time: 102 us
  Pallas kernels  96.5 us (95%)
  local copies, waits for them, and re-layouts  4.52 us (4%)
    pallas_call x1, Pallas kernels, local(): pl.pallas_call(functools.partial(kernel, nr, nc), out_shape=(jax.ShapeDty...  96.5 us
    unnamed x2, local copies, waits for them, and re-layouts  4.52 us

commit v1 on v0

v1 whole, which is shorter than its diff:
```python
import functools

import jax
import jax.numpy as jnp
from jax import lax
from jax.experimental import pallas as pl
from jax.experimental.pallas import tpu as pltpu
from jax.sharding import PartitionSpec as P

STEPS = 2
CHUNKS = 4
MESH = pl.DeviceIdType.MESH
F32 = jnp.float32
BF16 = jnp.bfloat16
LANES = 128


def rounded_sources(src, lanes, half, half_t):
    half[...] = src[...].astype(BF16)
    half_t[...] = (src[...].T * lanes).astype(BF16)


def row_scale(lanes, row_mask, step_size):
    block = row_mask.shape[0]
    for t in range(block // LANES):
        part = slice(t * LANES, (t + 1) * LANES)
        row_mask[part, :] = jnp.broadcast_to(lanes[:, part], (LANES, LANES)).T * step_size


def misfit_of(half, rec_half, observed):
    predicted = jnp.dot(half[...], rec_half, preferred_element_type=F32)
    return (observed.astype(F32) - predicted).astype(BF16)


def source_gradient(misfit, rec_half, live):
    return lax.dot_general(
        misfit, rec_half * live.astype(BF16), (((1,), (1,)), ((), ())),
        preferred_element_type=F32,
    )


def add_sources(dst, src, row_mask, grad):
    for h in range(src.shape[1] // LANES):
        part = slice(h * LANES, (h + 1) * LANES)
        dst[:, part] = src[:, part] + row_mask[...] * grad[:, part]


def sweep(rec_in, rec_out, observed, live_of, half, half_t, grad, step_size, done=None):
    rank, chunk = half_t.shape[0], rec_in.shape[1]
    chunks = rec_in.shape[0] // rank

    def front(q):
        rec_half = rec_in[q * rank:(q + 1) * rank, :].astype(BF16)
        return rec_half, misfit_of(half, rec_half, observed[:, q * chunk:(q + 1) * chunk])

    ahead = front(0)
    for q in range(chunks):
        rec_half, misfit = ahead
        if q + 1 < chunks:
            ahead = front(q + 1)
        rows = slice(q * rank, (q + 1) * rank)
        live = live_of(q)
        grad_rec = jnp.dot(half_t[...], misfit, preferred_element_type=F32)
        rec_out[rows, :] = rec_in[rows, :] + (step_size * live) * grad_rec
        grad_src = source_gradient(misfit, rec_half, live)
        if q == 0:
            grad[...] = grad_src
        else:
            grad[...] += grad_src
        if done is not None:
            done(q)


def main_kernel(nr, nc, tiles, row_live, col_live, order, src_in, rec_in, src_out, rec_out, tile_out,
                tile, rb, mids, outs, stage, grad, half, half_t, row_mask,
                in_sem, ring_send, ring_recv, a_send, a_recv, b_send, b_recv):
    strata, block, width = tiles.shape
    rank = src_out.shape[1]
    chunk = rb.shape[2]
    chunks = width // chunk
    sub = rank // nr
    step_size = 1.0 / (width + 2 * rank)
    r = lax.axis_index("row")
    c = lax.axis_index("col")
    cn = lax.rem(c + 1, nc)
    rn = lax.rem(r + (c + 1) // nc, nr)
    cp = lax.rem(c + nc - 1, nc)

    tile_of = [tile.at[s] for s in range(strata - 1)] + [tile_out]
    loads = [
        pltpu.make_async_copy(rec_in, stage, in_sem.at[strata]),
        pltpu.make_async_copy(src_in, src_out, in_sem.at[strata + 1]),
    ] + [pltpu.make_async_copy(tiles.at[s], tile_of[s], in_sem.at[s]) for s in range(strata)]
    for load in loads:
        load.start()

    barrier = pltpu.get_barrier_semaphore()
    for k in range(nr):
        pl.semaphore_signal(barrier, inc=1, device_id={"row": k, "col": cp}, device_id_type=MESH)
    for k in range(1, nr):
        pl.semaphore_signal(
            barrier, inc=1, device_id={"row": lax.rem(r + k, nr), "col": c}, device_id_type=MESH
        )

    def ring_copy(s, q):
        lane = 0 if s == 0 else 1
        rows = pl.ds(q * rank, rank)
        return pltpu.make_async_remote_copy(
            src_ref=rb.at[s, rows], dst_ref=rb.at[s + 1, rows],
            send_sem=ring_send.at[lane, q], recv_sem=ring_recv.at[lane, q],
            device_id={"row": rn, "col": cn}, device_id_type=MESH,
        )

    def a_copy(q, p, slot, static_q):
        return pltpu.make_async_remote_copy(
            src_ref=rb.at[1, pl.ds(q * rank + p * sub, sub)], dst_ref=mids[static_q].at[slot],
            send_sem=a_send.at[static_q, p], recv_sem=a_recv.at[static_q, slot],
            device_id={"row": p, "col": cn}, device_id_type=MESH,
        )

    def b_copy(q, to, p):
        return pltpu.make_async_remote_copy(
            src_ref=outs.at[q, to], dst_ref=rb.at[2, pl.ds(q * rank + p * sub, sub)],
            send_sem=b_send.at[q, to], recv_sem=b_recv.at[q, p],
            device_id={"row": to, "col": c}, device_id_type=MESH,
        )

    loads[0].wait()
    for q in range(chunks):
        rb[0, q * rank:(q + 1) * rank, :] = stage[q * chunk:(q + 1) * chunk, :].T
    loads[1].wait()

    for s in range(strata):
        lanes = row_live[s:s + 1, :].astype(F32)
        row_scale(lanes, row_mask, step_size)
        loads[s + 2].wait()
        for it in range(STEPS if s + 1 < strata else STEPS - 1):
            rounded_sources(src_out, lanes, half, half_t)

            def one(q, s=s, it=it):
                rows = pl.ds(pl.multiple_of(q * rank, rank), rank)
                cols = pl.ds(pl.multiple_of(q * chunk, chunk), chunk)
                if it == 0 and s == 2:
                    def wait_b(k, carry):
                        b_copy(q, r, lax.rem(r + k, nr)).wait_recv()
                        return carry
                    lax.fori_loop(1, nr, wait_b, 0)
                elif it == 0:
                    ring_copy(s - 1, q).wait_recv()
                rec = rb[s, rows, :]
                rec_half = rec.astype(BF16)
                live = col_live[s:s + 1, cols].astype(F32)
                misfit = misfit_of(half, rec_half, tile_of[s][:, cols])
                grad_rec = jnp.dot(half_t[...], misfit, preferred_element_type=F32)
                updated = rec + (step_size * live) * grad_rec
                if s + 1 == strata:
                    rec_out[rows, :] = updated
                else:
                    rb[s, rows, :] = updated
                grad_src = source_gradient(misfit, rec_half, live)

                @pl.when(q == 0)
                def _():
                    grad[...] = grad_src

                @pl.when(q > 0)
                def _():
                    grad[...] += grad_src

                if it == STEPS - 1 and s in (0, 2):
                    ring_copy(s, q).start()
                if it == STEPS - 1 and s == 1:
                    for static_q in range(chunks):
                        @pl.when(q == static_q)
                        def _(static_q=static_q):
                            def send_a(k, carry):
                                a_copy(static_q, lax.rem(r + k, nr), rn, static_q).start()
                                return carry
                            lax.fori_loop(0, nr, send_a, 0)

            if it == STEPS - 1 and s == 0:
                pl.semaphore_wait(barrier, 2 * nr - 1)
            if it == 0 and s == 0:
                sweep(rb.at[0], rb.at[0], tile_of[0],
                      lambda q: col_live[0:1, q * chunk:(q + 1) * chunk].astype(F32),
                      half, half_t, grad, step_size)
            else:
                def body(q, carry):
                    one(q)
                    return carry
                lax.fori_loop(0, chunks, body, 0)
            add_sources(src_out, src_out, row_mask, grad)
        if s == 1:
            for q in range(chunks):
                def wait_a(k, carry, q=q):
                    a_copy(q, 0, k, q).wait_recv()
                    return carry
                lax.fori_loop(0, nr, wait_a, 0)

                def send_b(k, carry, q=q):
                    to = lax.rem(r + k, nr)
                    outs[q, to] = mids[q][order[to]]
                    b_copy(q, to, r).start()
                    return carry
                lax.fori_loop(1, nr, send_b, 0)
                rb[2, pl.ds(pl.multiple_of(q * rank + r * sub, sub), sub), :] = mids[q][order[r]]

    for s in (0, 2):
        for q in range(chunks):
            ring_copy(s, q).wait_send()

    for q in range(chunks):
        def done_a(k, carry, q=q):
            a_copy(q, k, 0, q).wait_send()
            return carry
        lax.fori_loop(0, nr, done_a, 0)

        def done_b(k, carry, q=q):
            b_copy(q, lax.rem(r + k, nr), r).wait_send()
            return carry
        lax.fori_loop(1, nr, done_b, 0)


def last_kernel(src_in, rec_in, tile, row_live, col_live, sources, receivers,
                half, half_t, grad, row_mask, rec_new, turned, src_new, sem):
    block, width = tile.shape
    rank = src_in.shape[1]
    chunk = rec_in.shape[1]
    chunks = width // chunk
    step_size = 1.0 / (width + 2 * rank)
    s = row_live.shape[0] - 1
    lanes = row_live[s:s + 1, :].astype(F32)
    rounded_sources(src_in, lanes, half, half_t)
    row_scale(lanes, row_mask, step_size)
    copies = []

    def done(q):
        rows = slice(q * chunk, (q + 1) * chunk)
        turned[rows, :] = rec_new[q * rank:(q + 1) * rank, :].T
        if q % 2 == 1:
            pair = pl.ds((q - 1) * chunk, 2 * chunk)
            copies.append(pltpu.make_async_copy(turned.at[pair], receivers.at[pair], sem.at[q // 2]))
            copies[-1].start()

    sweep(rec_in, rec_new, tile,
          lambda q: col_live[s:s + 1, q * chunk:(q + 1) * chunk].astype(F32),
          half, half_t, grad, step_size, done)
    add_sources(src_new, src_in, row_mask, grad)
    copies.append(pltpu.make_async_copy(src_new, sources, sem.at[chunks // 2]))
    copies[-1].start()
    for copy in copies:
        copy.wait()


def local(nr, nc, tiles, row_live, col_live, row_order, source_init, receiver_init):
    strata, block, width = tiles.shape
    rank = source_init.shape[1]
    chunk = width // CHUNKS
    sub = rank // nr
    vmem = pl.BlockSpec(memory_space=pltpu.VMEM)
    anywhere = pl.BlockSpec(memory_space=pl.ANY)
    sources, receivers, tile = pl.pallas_call(
        functools.partial(main_kernel, nr, nc),
        out_shape=(
            pltpu.VMEM(source_init.shape, F32),
            pltpu.VMEM((CHUNKS * rank, chunk), F32),
            pltpu.VMEM((block, width), BF16),
        ),
        in_specs=[
            anywhere, vmem, vmem, pl.BlockSpec(memory_space=pltpu.SMEM), anywhere, anywhere,
        ],
        out_specs=(vmem, vmem, vmem),
        scratch_shapes=[
            pltpu.VMEM((strata - 1, block, width), BF16),
            pltpu.VMEM((strata, CHUNKS * rank, chunk), F32),
            [pltpu.VMEM((nr, sub, chunk), F32)] * CHUNKS,
            pltpu.VMEM((CHUNKS, nr, sub, chunk), F32),
            pltpu.VMEM(receiver_init.shape, F32),
            pltpu.VMEM((block, rank), F32),
            pltpu.VMEM((block, rank), BF16),
            pltpu.VMEM((rank, block), BF16),
            pltpu.VMEM((block, LANES), F32),
            pltpu.SemaphoreType.DMA((strata + 2,)),
            pltpu.SemaphoreType.DMA((2, CHUNKS)),
            pltpu.SemaphoreType.DMA((2, CHUNKS)),
            pltpu.SemaphoreType.DMA((CHUNKS, nr)),
            pltpu.SemaphoreType.DMA((CHUNKS, nr)),
            pltpu.SemaphoreType.DMA((CHUNKS, nr)),
            pltpu.SemaphoreType.DMA((CHUNKS, nr)),
        ],
        compiler_params=pltpu.CompilerParams(
            collective_id=0, has_side_effects=True, vmem_limit_bytes=56 * 1024 * 1024
        ),
    )(tiles, row_live, col_live, row_order, source_init, receiver_init)
    return pl.pallas_call(
        last_kernel,
        out_shape=(
            jax.ShapeDtypeStruct(source_init.shape, F32),
            jax.ShapeDtypeStruct(receiver_init.shape, F32),
        ),
        in_specs=[vmem] * 5,
        out_specs=(anywhere, anywhere),
        scratch_shapes=[
            pltpu.VMEM((block, rank), BF16),
            pltpu.VMEM((rank, block), BF16),
            pltpu.VMEM((block, rank), F32),
            pltpu.VMEM((block, LANES), F32),
            pltpu.VMEM((CHUNKS * rank, chunk), F32),
            pltpu.VMEM(receiver_init.shape, F32),
            pltpu.VMEM(source_init.shape, F32),
            pltpu.SemaphoreType.DMA((CHUNKS // 2 + 1,)),
        ],
        compiler_params=pltpu.CompilerParams(vmem_limit_bytes=40 * 1024 * 1024),
    )(sources, receivers, tile, row_live, col_live)


def solution(mesh):
    placed = (
        P(None, ("row", "col"), None),
        P(None, ("row", "col")),
        P(None, ("row", "col")),
        P(),
        P(("row", "col"), None),
        P(("row", "col"), None),
    )
    return jax.shard_map(
        functools.partial(local, mesh.shape["row"], mesh.shape["col"]),
        mesh=mesh,
        in_specs=placed,
        out_specs=(P(("row", "col"), None), P(("row", "col"), None)),
        check_vma=False,
    )
```

time: 102 us -> 93.3 us (0.915)
  local copies, waits for them, and re-layouts: 4.52 us -> 0.01 us
  Pallas kernels: 96.5 us -> 92.4 us
    unnamed x2 -> x4, local copies, waits for them, and re-layouts: 4.52 us -> 0.01 us
    pallas_call x1 -> x2, Pallas kernels: 96.5 us -> 92.4 us  [the longest x1 89.4 us: local(): pl.pallas_call(functools.partial(main_kernel, nr, nc), out_shape=(pltpu.V...]
where the time goes in v1:
time: 93.3 us; the launch traced here: 93.1 us
  Pallas kernels  92.4 us (99%)
    pallas_call x1, Pallas kernels, local(): pl.pallas_call(functools.partial(main_kernel, nr, nc), out_shape=(pltpu.V...  89.4 us
    pallas_call x1, Pallas kernels, local(): pl.pallas_call(last_kernel, out_shape=(jax.ShapeDtypeStruct(source_init.s...  3.04 us

profile of v1, /device:TPU:0, one launch (start us, length us, event | category | flops | bytes accessed | tf_op | source)
XLA Modules:
  0.0 93.1 jit_solution(16484269799953474759)
XLA Ops:
  0.6 0.0 copy-start.1
  0.6 0.0 copy-start
  0.7 89.4 %shard_map.77 = (f32[1024,256]{1,0:T(8,128)S(1)}, f32[1024,256]{1,0:T(8,128)S(1)}, bf16[1024,1024]{1,0:T(8,128)(2,1)S(1)}) custom-call(bf16[4,1024,1024]{2,1,0:T(8,128)(2,1)} %tiles.1, s32[4,1024]{1,0:T(4,128)} %row_live.3, s32[4,1024]{1,0:T(4,128)} %col_live.3, s32[8]{0:T(128)} %order.1, f32[1024,256]{1,0:T(8,128)} %src_in.1, f32[1024,256]{1,0:T(8,128)} %rec_in.1), custom_call_target="tpu_custom_call" | custom-call | tf_op jit(solution)/shard_map/pallas_call | solution.py:262
  90.0 0.0 copy-done.1
  90.0 0.0 copy-done
  90.0 3.0 %shard_map.78 = (f32[1024,256]{1,0:T(8,128)}, f32[1024,256]{1,0:T(8,128)}) custom-call(f32[1024,256]{1,0:T(8,128)S(1)} %get-tuple-element.5.src_in, f32[1024,256]{1,0:T(8,128)S(1)} %get-tuple-element.6.rec_in, bf16[1024,1024]{1,0:T(8,128)(2,1)S(1)} %get-tuple-element.7.tile, s32[4,1024]{1,0:T(4,128)S(1)} %copy-done, s32[4,1024]{1,0:T(4,128)S(1)} %copy-done.1), custom_call_target="tpu_custom_call" | custom-call | tf_op jit(solution)/shard_map/pallas_call | solution.py:295
Async XLA Ops:
  0.6 89.4 %copy-start.1 = (s32[4,1024]{1,0:T(4,128)S(1)}, s32[4,1024]{1,0:T(4,128)}, u32[]{:S(2)}) copy-start(s32[4,1024]{1,0:T(4,128)} %col_live.3) | copy-start | bytes 49156
  0.6 89.4 %copy-start = (s32[4,1024]{1,0:T(4,128)S(1)}, s32[4,1024]{1,0:T(4,128)}, u32[]{:S(2)}) copy-start(s32[4,1024]{1,0:T(4,128)} %row_live.3) | copy-start | bytes 49156
